TPU v7x, 32 devices: a whole 2x2x4 slice. The times are simulated.
32 devices in a mesh: section: 2 (over core), seq: 4 (over y, x), head: 4 (over z).
Axes of the slice: x: 2, y: 2, z: 4, core: 2. Of those that a mesh axis runs over, the one named last changes fastest.
Arguments:
- x_in: bfloat16 [2, 1024, 8192], P('section', 'seq', 'head'), may hold values from -6 to 6
- b_in: bfloat16 [2, 1024, 2048], P('section', 'seq', 'head'), may hold values from -6 to 6
- c_in: bfloat16 [2, 1024, 2048], P('section', 'seq', 'head'), may hold values from -6 to 6
- z_in: bfloat16 [2, 1024, 8192], P('section', 'seq', 'head'), may hold values from -6 to 6
- dt_raw: float32 [2, 128, 1024], P('section', 'head', 'seq'), may hold values from -5 to 5
- conv_x: float32 [2, 4, 8192], P('section', None, 'head'), may hold values from -3 to 3
- conv_b: float32 [2, 4, 2048], P('section', None, 'head'), may hold values from -3 to 3
- conv_c: float32 [2, 4, 2048], P('section', None, 'head'), may hold values from -3 to 3
- a_rate: float32 [2, 128], P('section', 'head'), may hold values from 0.0001 to 1
- dt_bias: float32 [2, 128], P('section', 'head'), may hold values from -3 to -0.5
- skip_d: float32 [2, 128], P('section', 'head'), may hold values from 0.5 to 2
- norm_gain: float32 [2, 8192], P('section', 'head'), may hold values from 0.25 to 1.75
- out_weight: bfloat16 [2, 8192, 8192], P('section', 'head', 'seq'), may hold values from -0.0625 to 0.0625
Outputs:
- mixed: bfloat16 [2, 1024, 8192], P('section', ('seq', 'head'))
All inputs are finite; a program needn't handle non-finite values.
Results may differ from a plain program's by a relative error of at most 0.007.
Values may be sent and summed in bfloat16 or wider, within the bound.
A program may use at most 128 MiB of HBM per device.

v0:
```python
import jax
import jax.numpy as jnp
from jax import lax
from jax.sharding import PartitionSpec as P

N = 256


epsilon = 1e-05


def passed_along(block, axis, distance):
    devices = range(lax.axis_size(axis))
    route = [(i - distance, i) for i in devices if i - distance in devices]
    return lax.ppermute(block, axis, route)


def entering(x, axis, combine, identity):
    size, place = (lax.axis_size(axis), lax.axis_index(axis))
    everything = jax.tree.map(lambda part: lax.all_gather(part, axis), x)
    start = jax.tree.map(
        lambda part, zero: jnp.broadcast_to(jnp.asarray(zero, part.dtype), part.shape), x, identity
    )

    def lap(k, before):
        reached = k < place
        new = combine(before, jax.tree.map(lambda part: part[k], everything))
        return jax.tree.map(lambda a, b: jnp.where(reached, a, b), new, before)

    return lax.fori_loop(0, size, lap, start)


def passed_along_2(block, axis, distance):
    devices = range(lax.axis_size(axis))
    route = [((i - distance) % len(devices), i) for i in devices]
    return lax.ppermute(block, axis, route)


def conv_silu(padded, kernel, length):
    kernel_taps = kernel.shape[0]
    summed = jnp.zeros((length, padded.shape[1]), jnp.float32)
    for offset in range(kernel_taps):
        summed = summed + kernel[offset] * padded[offset : offset + length].astype(jnp.float32)
    return jax.nn.silu(summed).astype(jnp.bfloat16)


def carry_combine(earlier, latter):
    return (earlier[0] * latter[0], latter[0][:, :, None, None] * earlier[1] + latter[1])


def per_device(
    x_in,
    b_in,
    c_in,
    z_in,
    dt_raw,
    conv_x,
    conv_b,
    conv_c,
    a_rate,
    dt_bias,
    skip_d,
    norm_gain,
    out_weight,
):
    x_local = x_in[0]
    b_local = b_in[0]
    c_local = c_in[0]
    length = x_local.shape[0]
    kernel_taps = conv_x.shape[1]
    x_cols = x_local.shape[1]
    b_cols = b_local.shape[1]
    edge_rows = jnp.concatenate(
        [
            x_local[length - kernel_taps + 1 :],
            b_local[length - kernel_taps + 1 :],
            c_local[length - kernel_taps + 1 :],
        ],
        axis=1,
    )
    before = passed_along(edge_rows, "seq", 1)
    x_conv = conv_silu(jnp.concatenate([before[:, :x_cols], x_local], axis=0), conv_x[0], length)
    b_conv = conv_silu(
        jnp.concatenate([before[:, x_cols : x_cols + b_cols], b_local], axis=0), conv_b[0], length
    )
    c_conv = conv_silu(
        jnp.concatenate([before[:, x_cols + b_cols :], c_local], axis=0), conv_c[0], length
    )
    head_count = dt_raw.shape[1]
    group_count = b_cols // N
    per_group = head_count // group_count
    head_dim = x_cols // head_count
    step_size = jax.nn.softplus(dt_raw[0] + dt_bias[0][:, None])
    log_decay = jnp.cumsum(-a_rate[0][:, None] * step_size, axis=1)
    x_groups = x_conv.reshape(length, group_count, per_group, head_dim)
    b_groups = b_conv.reshape(length, group_count, N)
    c_groups = c_conv.reshape(length, group_count, N)
    log_groups = log_decay.reshape(group_count, per_group, length)
    step_groups = step_size.reshape(group_count, per_group, length)
    scores = jnp.einsum("tgn,ugn->gtu", c_groups, b_groups, preferred_element_type=jnp.float32)
    causal = jnp.arange(length)[:, None] >= jnp.arange(length)[None, :]
    spread_log = log_groups[:, :, :, None] - log_groups[:, :, None, :]
    damping = jnp.where(causal, jnp.exp(jnp.minimum(spread_log, 0.0)), 0.0)
    weights = (damping * step_groups[:, :, None, :] * scores[:, None]).astype(jnp.bfloat16)
    inside = jnp.einsum("gjtu,ugjp->tgjp", weights, x_groups, preferred_element_type=jnp.float32)
    to_end = jnp.exp(log_groups[:, :, -1:] - log_groups) * step_groups
    x_weighted = (
        x_groups.astype(jnp.float32) * jnp.transpose(to_end, (2, 0, 1))[..., None]
    ).astype(jnp.bfloat16)
    block_sum = jnp.einsum(
        "ugjp,ugn->gjpn", x_weighted, b_groups, preferred_element_type=jnp.float32
    )
    block_decay = jnp.exp(log_groups[:, :, -1])
    identity = (jnp.ones_like(block_decay), jnp.zeros_like(block_sum))
    carried_decay, carried = entering((block_decay, block_sum), "seq", carry_combine, identity)
    carried_b = carried.astype(jnp.bfloat16)
    outside = jnp.einsum("tgn,gjpn->tgjp", c_groups, carried_b, preferred_element_type=jnp.float32)
    outside = outside * jnp.transpose(jnp.exp(log_groups), (2, 0, 1))[..., None]
    skip_term = skip_d[0].reshape(group_count, per_group)
    out_ssm = inside + outside + skip_term[None, :, :, None] * x_groups.astype(jnp.float32)
    gate_act = jax.nn.silu(z_in[0].astype(jnp.float32)).reshape(
        length, group_count, per_group * head_dim
    )
    gated = out_ssm.reshape(length, group_count, per_group * head_dim) * gate_act
    inverse_rms = lax.rsqrt(jnp.mean(gated * gated, axis=2, keepdims=True) + epsilon)
    hidden = ((gated * inverse_rms).reshape(length, x_cols) * norm_gain[0]).astype(jnp.bfloat16)
    local_weight = out_weight[0]
    terms = jnp.dot(
        lax.all_gather(hidden, "seq", axis=0, tiled=True),
        local_weight,
        preferred_element_type=jnp.float32,
    )
    shards = lax.axis_size("seq")
    terms = terms.reshape(shards, length, local_weight.shape[1])
    summed = lax.psum_scatter(terms, "head", scatter_dimension=1, tiled=True).astype(jnp.bfloat16)
    spread = lax.all_to_all(summed, "seq", split_axis=0, concat_axis=2, tiled=True)
    mixed = spread.reshape(spread.shape[1], spread.shape[2])
    passed = passed_along_2(mixed, "section", 1)
    return passed[None]


def solution(mesh):
    return jax.shard_map(
        per_device,
        mesh=mesh,
        in_specs=(
            P("section", "seq", "head"),
            P("section", "seq", "head"),
            P("section", "seq", "head"),
            P("section", "seq", "head"),
            P("section", "head", "seq"),
            P("section", None, "head"),
            P("section", None, "head"),
            P("section", None, "head"),
            P("section", "head"),
            P("section", "head"),
            P("section", "head"),
            P("section", "head"),
            P("section", "head", "seq"),
        ),
        out_specs=P("section", ("seq", "head"), None),
        check_vma=False,
    )
```

profile of v0, /device:TPU:0, one launch (start us, length us, event | category | flops | bytes accessed | tf_op | source)
XLA Modules:
  0.0 381.0 jit_solution(10214932732232863792)
XLA Ops:
  8.1 4.9 %collective-permute-start = (bf16[3,3072]{1,0:T(4,128)(2,1)S(1)}, bf16[3,3072]{1,0:T(4,128)(2,1)S(1)}, u32[]{:S(2)}, u32[]{:S(2)}) collective-permute-start(bf16[3,3072]{1,0:T(4,128)(2,1)S(1)} %pad_maximum_fusion.3), channel_id=1, source_target_pairs={{0,4},{4,8},{8,12},{1,5},{5,9},{9,13},{2,6},{6,10},{10,14},{3,7},{... | collective-permute-start | bytes 55304 | tf_op jit(solution)/shard_map/ppermute | solution.py:15
  21.6 1.9 multiply_convert_fusion.5
  23.6 1.5 multiply_convert_fusion.2
  25.6 1.8 fusion.22
  28.9 1.6 copy.66
  30.6 8.1 %all-gather = f32[8,16,1]{1,2,0:T(1,128)S(1)} all-gather(f32[2,16,1]{1,2,0:T(1,128)S(1)} %bitcast.134), channel_id=2, replica_groups=mesh['section'=2,'seq'=4,'head'=4] {'seq'}, dimensions={0}, use_global_device_ids=true | all-gather | bytes 640 | tf_op jit(solution)/shard_map/all_gather | solution.py:20
  38.7 2.5 multiply_convert_fusion.6
  41.2 1.7 reshape.164
  43.0 2.0 fusion.31
  45.0 70.4 %all-gather.7.cloned.1.call-done = f32[8,16,64,256]{3,2,1,0:T(8,128)} async-done(((f32[2,16,64,256]{3,2,1,0:T(8,128)}), f32[8,16,64,256]{3,2,1,0:T(8,128)}) %all-gather.7.cloned.1.call-update) | async-done | bytes 8388624 | tf_op jit(solution)/shard_map/all_gather | solution.py:20
  115.4 8.6 %while.14 = (s32[]{:T(128)}, f32[2,16,64,256]{3,2,1,0:T(8,128)S(1)}, s32[]{:T(128)}, f32[4,2,16]{2,1,0:T(2,128)S(1)}, f32[4,2,16,64,256]{4,3,2,1,0:T(8,128)}, /*index=5*/s32[]{:T(128)}, s32[]{:T(128)}) while((s32[]{:T(128)}, f32[2,16,64,256]{3,2,1,0:T(8,128)S(1)}, s32[]{:T(128)}, f32[4,2,16]{2,1,0:T(2,128)S(1)}, ...), condition=%wide.region_3.4_spmd.clone, body=%wide.region_2.3_spmd.clone.sunk | while | flops 2097156 | bytes 6291945 | solution.py:30
  115.4 2.1 fusion.47
  117.6 2.1 fusion.47
  119.7 2.1 fusion.47
  121.9 2.1 fusion.47
  126.0 4.5 %multiply_reduce_fusion = (f32[256,2]{0,1:T(2,128)S(1)}, f32[256,2,16,64]{0,3,2,1:T(8,128)}) fusion(f32[256,2,16,64]{0,3,2,1:T(8,128)S(1)} %bitcast.109, bf16[256,2,16,64]{0,3,2,1:T(8,128)(2,1)S(1)} %bitcast.104, f32[2,16]{1,0:T(2,128)S(1)} %copy-done.11, f32[256,2,16]{0,2,1:T(8,128)S(1)} %copy-done.7, f32[2,16,64,256]{3,2,1,0:T(8,128)S(1)} %fusion.24, ...), kind=kOutput, calls=%fused_computation.27 | convolution fusion | flops 287309312 | bytes 8030336 | tf_op jit(solution)/shard_map/gjtu,ugjp->tgjp/dot_general | solution.py:105
  132.1 2.9 copy.65
  135.0 3.3 fusion.19
  138.4 52.7 %all-gather.5.cloned.1.call-done = bf16[1024,2048]{1,0:T(8,128)(2,1)} async-done(((bf16[256,2048]{1,0:T(8,128)(2,1)}), bf16[1024,2048]{1,0:T(8,128)(2,1)}) %all-gather.5.cloned.1.call-update) | async-done | bytes 4194320 | tf_op jit(solution)/shard_map/all_gather | solution.py:129
  191.1 14.5 %fusion.1 = f32[4,256,2048]{2,1,0:T(8,128)} fusion(bf16[4,256,2048]{2,1,0:T(8,128)(2,1)} %bitcast.136, bf16[1,2048,2048]{2,1,0:T(8,128)(2,1)} %param.27), kind=kOutput, calls=%fused_computation.3 | convolution fusion | flops 8589934592 | bytes 20971520 | tf_op jit(solution)/shard_map/dot_general | solution.py:128
  205.6 144.8 %reduce-scatter.2.cloned.1.call-done = f32[4,64,2048]{2,1,0:T(8,128)} async-done(((f32[4,256,2048]{2,1,0:T(8,128)}), f32[4,64,2048]{2,1,0:T(8,128)}) %reduce-scatter.2.cloned.1.call-update) | async-done | bytes 2097168 | tf_op jit(solution)/shard_map/reduce_scatter | solution.py:135
  350.4 1.7 convert_element_type.102
  352.2 17.2 %all_to_all.15 = bf16[4,64,2048]{2,1,0:T(8,128)(2,1)S(1)} all-to-all(bf16[4,64,2048]{2,1,0:T(8,128)(2,1)S(1)} %convert_element_type.102), channel_id=1, replica_groups=mesh['section'=2,'seq'=4,'head'=4] {'seq'}, dimensions={0} | all-to-all | bytes 2097152 | tf_op jit(solution)/shard_map/all_to_all | solution.py:136
  370.9 2.6 collective-permute-done.1
  (75 shorter events, 18.4 us)
Async XLA Ops:
  6.5 17.0 %copy-start.4 = (bf16[1,256,2048]{2,1,0:T(8,128)(2,1)S(1)}, bf16[1,256,2048]{2,1,0:T(8,128)(2,1)}, u32[]{:S(2)}) copy-start(bf16[1,256,2048]{2,1,0:T(8,128)(2,1)} %param.15) | copy-start | bytes 3145732
  6.5 108.8 %all-gather.7.cloned.1.call-start = ((), (), s32[]{:S(2)}) async-start(), calls=%async_computation.4 | async-start | bytes 10485760 | tf_op jit(solution)/shard_map/all_gather | solution.py:20
  8.1 13.4 %collective-permute-start = (bf16[3,3072]{1,0:T(4,128)(2,1)S(1)}, bf16[3,3072]{1,0:T(4,128)(2,1)S(1)}, u32[]{:S(2)}, u32[]{:S(2)}) collective-permute-start(bf16[3,3072]{1,0:T(4,128)(2,1)S(1)} %pad_maximum_fusion.3), channel_id=1, source_target_pairs={{0,4},{4,8},{8,12},{1,5},{5,9},{9,13},{2,6},{6,10},{10,14},{3,7},{... | collective-permute-start | bytes 55304 | tf_op jit(solution)/shard_map/ppermute | solution.py:15
  25.6 1.9 copy-start.1
  25.6 1.9 copy-start.10
  25.6 3.3 copy-start
  27.4 11.3 %copy-start.9 = (f32[1,4,512]{2,1,0:T(4,128)S(1)}, f32[1,4,512]{2,1,0:T(4,128)}, u32[]{:S(2)}) copy-start(f32[1,4,512]{2,1,0:T(4,128)} %param.22) | copy-start | bytes 24580
  27.4 163.6 %all-gather.5.cloned.1.call-start = ((), (), s32[]{:S(2)}) async-start(), calls=%async_computation.2 | async-start | bytes 5242880 | tf_op jit(solution)/shard_map/all_gather | solution.py:129
  115.4 8.6 %copy-start.5 = (bf16[256,2,256]{2,1,0:T(2,128)(2,1)S(1)}, bf16[256,2,256]{2,1,0:T(2,128)(2,1)}, u32[]{:S(2)}) copy-start(bf16[256,2,256]{2,1,0:T(2,128)(2,1)} %reshape.164) | copy-start | bytes 786436
  124.0 1.2 copy-start.2
  124.0 1.9 copy-start.3
  124.0 2.0 copy-start.6
  124.0 2.0 copy-start.7
  124.0 2.0 copy-start.11
  132.1 2.9 copy-start.8
  138.4 212.1 %reduce-scatter.2.cloned.1.call-start = ((), (), s32[]{:S(2)}) async-start(), calls=%async_computation.3 | async-start | bytes 10485760 | tf_op jit(solution)/shard_map/reduce_scatter | solution.py:135
  370.8 2.7 collective-permute-start.1
Sparse Core Ops, SparseCore 0:
  27.5 87.7 all-gather.6
  138.5 52.5 all-gather.4
  205.8 144.6 reduce-scatter.1
where the time goes:
time: 382 us; the launch traced here: 381 us
  waiting for transfers between devices  271 us (71%)
  blocking collectives  25.3 us (7%)
  other arithmetic  25 us (7%)
  matrix products  23.3 us (6%)
  local copies, waits for them, and re-layouts  18.4 us (5%)
  between operations  13.4 us (4%)
  starting transfers between devices  5.03 us (1%)
    reduce_scatter x1, waiting for transfers between devices, per_device(): lax.psum_scatter(terms, 'head', scatter_dimension=1, tiled=True)  145 us
    all_gather x1, waiting for transfers between devices, entering(): everything = jax.tree.map(lambda part: lax.all_gather(part, axis), x)  70.4 us
    all_gather x1, waiting for transfers between devices, per_device(): lax.all_gather(hidden, 'seq', axis=0, tiled=True)  52.7 us
    all_to_all x1, blocking collectives, per_device(): lax.all_to_all(summed, 'seq', split_axis=0, concat_axis=2, tiled=True)  17.2 us
    dot_general x1, matrix products, per_device(): jnp.dot(lax.all_gather(hidden, 'seq', axis=0, tiled=True), local_weight,...  14.5 us
    select_n x4, other arithmetic, lap(): return jax.tree.map(lambda a, b: jnp.where(reached, a, b), new, before)  8.45 us
    all_gather x1, blocking collectives, entering(): everything = jax.tree.map(lambda part: lax.all_gather(part, axis), x)  8.08 us
  transfers between devices with their start and end apart: 5, of which 4 were waited for; matrix products, arithmetic and copies ran while one was open for 5% of the time, Pallas kernels for 0%

commit v1 on v0

--- a/solution.py
+++ b/solution.py
@@ -15,19 +15,15 @@
     return lax.ppermute(block, axis, route)
 
 
-def entering(x, axis, combine, identity):
+def entering(decay, block, axis):
     size, place = (lax.axis_size(axis), lax.axis_index(axis))
-    everything = jax.tree.map(lambda part: lax.all_gather(part, axis), x)
-    start = jax.tree.map(
-        lambda part, zero: jnp.broadcast_to(jnp.asarray(zero, part.dtype), part.shape), x, identity
-    )
-
-    def lap(k, before):
-        reached = k < place
-        new = combine(before, jax.tree.map(lambda part: part[k], everything))
-        return jax.tree.map(lambda a, b: jnp.where(reached, a, b), new, before)
-
-    return lax.fori_loop(0, size, lap, start)
+    decays = lax.all_gather(decay, axis)
+    blocks = lax.all_gather(block.astype(jnp.bfloat16), axis)
+    carried = jnp.zeros_like(block)
+    for k in range(size - 1):
+        after = decays[k][:, :, None, None] * carried + blocks[k].astype(jnp.float32)
+        carried = jnp.where(k < place, after, carried)
+    return carried
 
 
 def passed_along_2(block, axis, distance):
@@ -42,10 +38,6 @@
     for offset in range(kernel_taps):
         summed = summed + kernel[offset] * padded[offset : offset + length].astype(jnp.float32)
     return jax.nn.silu(summed).astype(jnp.bfloat16)
-
-
-def carry_combine(earlier, latter):
-    return (earlier[0] * latter[0], latter[0][:, :, None, None] * earlier[1] + latter[1])
 
 
 def per_device(
@@ -111,8 +103,7 @@
         "ugjp,ugn->gjpn", x_weighted, b_groups, preferred_element_type=jnp.float32
     )
     block_decay = jnp.exp(log_groups[:, :, -1])
-    identity = (jnp.ones_like(block_decay), jnp.zeros_like(block_sum))
-    carried_decay, carried = entering((block_decay, block_sum), "seq", carry_combine, identity)
+    carried = entering(block_decay, block_sum, "seq")
     carried_b = carried.astype(jnp.bfloat16)
     outside = jnp.einsum("tgn,gjpn->tgjp", c_groups, carried_b, preferred_element_type=jnp.float32)
     outside = outside * jnp.transpose(jnp.exp(log_groups), (2, 0, 1))[..., None]
@@ -131,8 +122,8 @@
         preferred_element_type=jnp.float32,
     )
     shards = lax.axis_size("seq")
-    terms = terms.reshape(shards, length, local_weight.shape[1])
-    summed = lax.psum_scatter(terms, "head", scatter_dimension=1, tiled=True).astype(jnp.bfloat16)
+    terms = terms.astype(jnp.bfloat16).reshape(shards, length, local_weight.shape[1])
+    summed = lax.psum_scatter(terms, "head", scatter_dimension=1, tiled=True)
     spread = lax.all_to_all(summed, "seq", split_axis=0, concat_axis=2, tiled=True)
     mixed = spread.reshape(spread.shape[1], spread.shape[2])
     passed = passed_along_2(mixed, "section", 1)

time: 382 us -> 266 us (0.70)
  waiting for transfers between devices: 271 us -> 174 us
  other arithmetic: 25 us -> 11 us
  local copies, waits for them, and re-layouts: 18.4 us -> 13.5 us
    reduce_scatter x1, waiting for transfers between devices: 145 us -> 77 us  [per_device(): summed = lax.psum_scatter(terms, 'head', scatter_dimension=1, tiled=True)]
    all_gather x1, waiting for transfers between devices: 70.4 us -> 41.8 us  [entering(): blocks = lax.all_gather(block.astype(jnp.bfloat16), axis)]
    select_n x4 -> x0, other arithmetic: 8.45 us -> none  [lap(): return jax.tree.map(lambda a, b: jnp.where(reached, a, b), new, before)]
  transfers between devices with their start and end apart: 5 -> 5, of which waited for: 4 -> 4; matrix products, arithmetic and copies ran while one was open for 5% -> 4% of each run, Pallas kernels for 0% -> 0%
where the time goes in v1:
time: 266 us
  waiting for transfers between devices  174 us (65%)
  blocking collectives  25.7 us (10%)
  matrix products  22.9 us (9%)
  local copies, waits for them, and re-layouts  13.5 us (5%)
  between operations  13.4 us (5%)
  other arithmetic  11 us (4%)
  starting transfers between devices  5.03 us (2%)
    reduce_scatter x1, waiting for transfers between devices, per_device(): summed = lax.psum_scatter(terms, 'head', scatter_dimension=1, tiled=True)  77 us
    all_gather x1, waiting for transfers between devices, per_device(): lax.all_gather(hidden, 'seq', axis=0, tiled=True)  52.7 us
    all_gather x1, waiting for transfers between devices, entering(): blocks = lax.all_gather(block.astype(jnp.bfloat16), axis)  41.8 us
    all_to_all x1, blocking collectives, per_device(): lax.all_to_all(summed, 'seq', split_axis=0, concat_axis=2, tiled=True)  17.6 us
    dot_general x1, matrix products, per_device(): jnp.dot(lax.all_gather(hidden, 'seq', axis=0, tiled=True), local_weight,...  13.8 us
    all_gather x1, blocking collectives, entering(): decays = lax.all_gather(decay, axis)  8.08 us
  transfers between devices with their start and end apart: 5, of which 4 were waited for; matrix products, arithmetic and copies ran while one was open for 4% of the time, Pallas kernels for 0%

profile of v1, /device:TPU:0, one launch (start us, length us, event | category | flops | bytes accessed | tf_op | source)
XLA Modules:
  0.0 265.6 jit_solution(9218574246040160207)
XLA Ops:
  6.5 0.9 slice_bitcast_fusion
  8.1 4.9 %collective-permute-start = (bf16[3,3072]{1,0:T(4,128)(2,1)S(1)}, bf16[3,3072]{1,0:T(4,128)(2,1)S(1)}, u32[]{:S(2)}, u32[]{:S(2)}) collective-permute-start(bf16[3,3072]{1,0:T(4,128)(2,1)S(1)} %pad_maximum_fusion.3), channel_id=1, source_target_pairs={{0,4},{4,8},{8,12},{1,5},{5,9},{9,13},{2,6},{6,10},{10,14},{3,7},{... | collective-permute-start | bytes 55304 | tf_op jit(solution)/shard_map/ppermute | solution.py:15
  14.2 1.3 reduce.9
  18.2 0.9 fusion.50
  19.2 1.4 multiply_bitcast_fusion
  20.6 0.9 fusion.53
  21.4 1.9 multiply_convert_fusion.5
  23.5 1.5 multiply_convert_fusion.2
  25.5 1.4 convolution_convert_fusion
  27.8 1.6 copy.67
  29.4 8.1 %all-gather = f32[8,16,1]{1,2,0:T(1,128)S(1)} all-gather(f32[2,16,1]{1,2,0:T(1,128)S(1)} %bitcast.125), channel_id=2, replica_groups=mesh['section'=2,'seq'=4,'head'=4] {'seq'}, dimensions={0}, use_global_device_ids=true | all-gather | bytes 640 | tf_op jit(solution)/shard_map/all_gather | solution.py:20
  38.2 41.8 %all-gather.7.cloned.1.call-done = bf16[8,16,64,256]{3,2,1,0:T(8,128)(2,1)} async-done(((bf16[2,16,64,256]{3,2,1,0:T(8,128)(2,1)}), bf16[8,16,64,256]{3,2,1,0:T(8,128)(2,1)}) %all-gather.7.cloned.1.call-update) | async-done | bytes 4194320 | tf_op jit(solution)/shard_map/all_gather | solution.py:21
  80.0 3.0 %fusion.31 = f32[2,16,64,256]{3,2,1,0:T(8,128)S(1)} fusion(bf16[8,16,64,256]{3,2,1,0:T(8,128)(2,1)} %all-gather.7.cloned.1.call-done, f32[2,16]{1,0:T(2,128)S(1)} %bitcast.128, f32[2,16]{1,0:T(2,128)S(1)} %bitcast.127, f32[2,16]{1,0:T(2,128)S(1)} %bitcast.126, pred[]{:T(512)S(6)} %gt.11, pred[]{:T(512)S(6)} %gt.10, pred[]{:T(512)S(6)} %gt.9, ...), kind=kOutput, calls=%fused_computation.43 | convolution fusion | flops 274726912 | bytes 5505411 | tf_op jit(solution)/shard_map/tgn,gjpn->tgjp/dot_general | solution.py:108
  83.0 4.5 %multiply_reduce_fusion = (f32[256,2]{0,1:T(2,128)S(1)}, f32[256,2,16,64]{0,3,2,1:T(8,128)}) fusion(f32[256,2,16,64]{0,3,2,1:T(8,128)S(1)} %bitcast.99, bf16[256,2,16,64]{0,3,2,1:T(8,128)(2,1)S(1)} %bitcast.103, f32[2,16]{1,0:T(2,128)S(1)} %mul.316, f32[256,2,16]{0,2,1:T(8,128)S(1)} %copy-done.4, f32[2,16,64,256]{3,2,1,0:T(8,128)S(1)} %fusion.31, ...), kind=kOutput, calls=%fused_computation.33 | convolution fusion | flops 287309312 | bytes 8030336 | tf_op jit(solution)/shard_map/gjtu,ugjp->tgjp/dot_general | solution.py:97
  87.5 1.9 copy.66
  90.2 0.9 copy.79
  91.1 1.8 fusion.26
  92.9 52.7 %all-gather.5.cloned.1.call-done = bf16[1024,2048]{1,0:T(8,128)(2,1)} async-done(((bf16[256,2048]{1,0:T(8,128)(2,1)}), bf16[1024,2048]{1,0:T(8,128)(2,1)}) %all-gather.5.cloned.1.call-update) | async-done | bytes 4194320 | tf_op jit(solution)/shard_map/all_gather | solution.py:120
  145.6 13.8 %fusion.9 = bf16[1024,2048]{1,0:T(8,128)(2,1)} fusion(bf16[1024,2048]{1,0:T(8,128)(2,1)} %all-gather.5.cloned.1.call-done, bf16[1,2048,2048]{2,1,0:T(8,128)(2,1)} %param.25), kind=kOutput, calls=%fused_computation.10 | convolution fusion | flops 8592031744 | bytes 16777216 | tf_op jit(solution)/shard_map/dot_general | solution.py:119
  159.4 77.0 %reduce-scatter.2.cloned.1.call-done = bf16[4,64,2048]{2,1,0:T(8,128)(2,1)} async-done(((bf16[4,256,2048]{2,1,0:T(8,128)(2,1)}), bf16[4,64,2048]{2,1,0:T(8,128)(2,1)}) %reduce-scatter.2.cloned.1.call-update) | async-done | bytes 1048592 | tf_op jit(solution)/shard_map/reduce_scatter | solution.py:126
  236.4 17.6 %all_to_all.15 = bf16[4,64,2048]{2,1,0:T(8,128)(2,1)S(1)} all-to-all(bf16[4,64,2048]{2,1,0:T(8,128)(2,1)} %reduce-scatter.2.cloned.1.call-done), channel_id=1, replica_groups=mesh['section'=2,'seq'=4,'head'=4] {'seq'}, dimensions={0} | all-to-all | bytes 2097152 | tf_op jit(solution)/shard_map/all_to_all | solution.py:127
  254.0 0.8 copy.69
  255.5 2.6 collective-permute-done.1
  258.1 1.0 copy.97
  (57 shorter events, 8.3 us)
Async XLA Ops:
  6.5 16.9 %copy-start.2 = (bf16[1,256,2048]{2,1,0:T(8,128)(2,1)S(1)}, bf16[1,256,2048]{2,1,0:T(8,128)(2,1)}, u32[]{:S(2)}) copy-start(bf16[1,256,2048]{2,1,0:T(8,128)(2,1)} %param.13) | copy-start | bytes 3145732
  6.5 73.5 %all-gather.7.cloned.1.call-start = ((), (), s32[]{:S(2)}) async-start(), calls=%async_computation.4 | async-start | bytes 5242880 | tf_op jit(solution)/shard_map/all_gather | solution.py:21
  8.1 13.3 %collective-permute-start = (bf16[3,3072]{1,0:T(4,128)(2,1)S(1)}, bf16[3,3072]{1,0:T(4,128)(2,1)S(1)}, u32[]{:S(2)}, u32[]{:S(2)}) collective-permute-start(bf16[3,3072]{1,0:T(4,128)(2,1)S(1)} %pad_maximum_fusion.3), channel_id=1, source_target_pairs={{0,4},{4,8},{8,12},{1,5},{5,9},{9,13},{2,6},{6,10},{10,14},{3,7},{... | collective-permute-start | bytes 55304 | tf_op jit(solution)/shard_map/ppermute | solution.py:15
  25.5 1.6 copy-start.7
  25.5 2.3 copy-start
  26.9 10.6 %copy-start.6 = (f32[1,4,512]{2,1,0:T(4,128)S(1)}, f32[1,4,512]{2,1,0:T(4,128)}, u32[]{:S(2)}) copy-start(f32[1,4,512]{2,1,0:T(4,128)} %param.20) | copy-start | bytes 24580
  26.9 10.6 %copy-start.3 = (bf16[1,256,512]{2,1,0:T(8,128)(2,1)S(1)}, bf16[1,256,512]{2,1,0:T(8,128)(2,1)}, u32[]{:S(2)}) copy-start(bf16[1,256,512]{2,1,0:T(8,128)(2,1)} %param.15) | copy-start | bytes 786436
  27.0 118.6 %all-gather.5.cloned.1.call-start = ((), (), s32[]{:S(2)}) async-start(), calls=%async_computation.2 | async-start | bytes 5242880 | tf_op jit(solution)/shard_map/all_gather | solution.py:120
  80.0 3.0 %copy-start.1 = (f32[1,256,2048]{1,2,0:T(8,128)S(1)}, f32[1,256,2048]{1,2,0:T(8,128)}, u32[]{:S(2)}) copy-start(f32[1,256,2048]{1,2,0:T(8,128)} %copy.67) | copy-start | bytes 6291460
  80.0 3.0 %copy-start.4 = (f32[256,2,16]{0,2,1:T(8,128)S(1)}, f32[256,2,16]{0,2,1:T(8,128)}, u32[]{:S(2)}) copy-start(f32[256,2,16]{0,2,1:T(8,128)} %get-tuple-element.7) | copy-start | bytes 98308
  90.2 0.9 copy-start.5
  92.9 143.5 %reduce-scatter.2.cloned.1.call-start = ((), (), s32[]{:S(2)}) async-start(), calls=%async_computation.3 | async-start | bytes 5242880 | tf_op jit(solution)/shard_map/reduce_scatter | solution.py:126
  255.4 2.7 %collective-permute-start.1 = (bf16[64,8192]{1,0:T(8,128)(2,1)S(1)}, bf16[64,8192]{1,0:T(8,128)(2,1)S(1)}, u32[]{:S(2)}, u32[]{:S(2)}) collective-permute-start(bf16[64,8192]{1,0:T(8,128)(2,1)S(1)} %bitcast.104), channel_id=1, source_target_pairs={{16,0},{0,16},{17,1},{1,17},{18,2},{2,18},{19,3},{3,19},{20,4},{4,... | collective-permute-start | bytes 3145736 | tf_op jit(solution)/shard_map/ppermute | solution.py:32
Sparse Core Ops, SparseCore 0:
  27.1 52.8 all-gather.6
  93.0 52.5 all-gather.4
  159.6 76.7 reduce-scatter.1

commit v2 on v1

--- a/solution.py
+++ b/solution.py
@@ -1,6 +1,10 @@
+import functools
+
 import jax
 import jax.numpy as jnp
 from jax import lax
+from jax.experimental import pallas as pl
+from jax.experimental.pallas import tpu as pltpu
 from jax.sharding import PartitionSpec as P
 
 N = 256
@@ -26,10 +30,141 @@
     return carried
 
 
-def passed_along_2(block, axis, distance):
-    devices = range(lax.axis_size(axis))
-    route = [((i - distance) % len(devices), i) for i in devices]
-    return lax.ppermute(block, axis, route)
+def partner(place, bits):
+    bit = 1
+    while bit <= bits:
+        if bits & bit:
+            place = place + bit - 2 * bit * ((place // bit) % 2)
+        bit *= 2
+    return place
+
+
+def project_kernel(
+    sizes, hid, weight, out, w_buf, got, part, landed, summed,
+    w_sem, ag_send, ag_recv, z_send, z_recv, o_send, o_recv,
+):
+    sections, shards, heads = sizes
+    halves, count, _ = hid.shape
+    rows, width = part.shape[3], part.shape[4]
+    tile = min(512, width)
+    here_s, here_h = lax.axis_index("seq"), lax.axis_index("head")
+    other = lax.rem(lax.axis_index("section") + 1, sections)
+    load = pltpu.make_async_copy(weight, w_buf, w_sem)
+    load.start()
+    barrier = pltpu.get_barrier_semaphore()
+    for d in range(shards):
+        if d:
+            pl.semaphore_signal(barrier, inc=1, device_id={"seq": partner(here_s, d)})
+        pl.semaphore_signal(
+            barrier, inc=1, device_id={"section": other, "seq": partner(here_s, d)}
+        )
+    for e in range(1, heads):
+        pl.semaphore_signal(barrier, inc=1, device_id={"head": partner(here_h, e)})
+    pl.semaphore_wait(barrier, 2 * shards - 1 + heads - 1)
+
+    def gather(q, d):
+        return pltpu.make_async_remote_copy(
+            hid.at[q], got.at[q, d - 1], ag_send.at[q, d], ag_recv.at[q, d],
+            device_id={"seq": partner(here_s, d)},
+        )
+
+    def exchange(q, d, e):
+        return pltpu.make_async_remote_copy(
+            part.at[q, d, partner(here_h, e)], landed.at[q, d, e - 1],
+            z_send.at[q, d, e], z_recv.at[q, d, e],
+            device_id={"head": partner(here_h, e)},
+        )
+
+    def deliver(q, d):
+        return pltpu.make_async_remote_copy(
+            summed.at[q, d], out.at[q, here_s], o_send.at[q, d], o_recv.at[q, d],
+            device_id={"section": other, "seq": partner(here_s, d)},
+        )
+
+    for q in range(halves):
+        for d in range(1, shards):
+            gather(q, d).start()
+    load.wait()
+
+    def multiply(q, d):
+        rows_in = hid.at[q] if d == 0 else got.at[q, d - 1]
+
+        def one(i, _):
+            cols = pl.ds(pl.multiple_of(i * tile, tile), tile)
+            terms = jnp.dot(rows_in[...], w_buf[:, cols], preferred_element_type=jnp.float32)
+            part[q, d, :, :, cols] = terms.astype(jnp.bfloat16).reshape(heads, rows, tile)
+            return 0
+
+        lax.fori_loop(0, width // tile, one, 0)
+
+    def finish(q, d):
+        total = part[q, d, here_h].astype(jnp.float32)
+        for e in range(1, heads):
+            exchange(q, d, e).wait_recv()
+            total = total + landed[q, d, e - 1].astype(jnp.float32)
+        summed[q, d] = total.astype(jnp.bfloat16)
+        deliver(q, d).start()
+
+    units = [(q, 0) for q in range(halves)]
+    units += [(q, d) for q in range(halves) for d in range(1, shards)]
+    lag = 2
+    for n, (q, d) in enumerate(units):
+        if d:
+            gather(q, d).wait_recv()
+        multiply(q, d)
+        for e in range(1, heads):
+            exchange(q, d, e).start()
+        if n >= lag:
+            finish(*units[n - lag])
+    for unit in units[len(units) - lag :]:
+        finish(*unit)
+    for q, d in units:
+        if d:
+            gather(q, d).wait_send()
+        for e in range(1, heads):
+            exchange(q, d, e).wait_send()
+        deliver(q, d).wait_send()
+        pltpu.make_async_remote_copy(
+            summed.at[q, d], out.at[q, partner(here_s, d)], o_send.at[q, d], o_recv.at[q, d],
+            device_id={"section": other, "seq": partner(here_s, d)},
+        ).wait_recv()
+
+
+def project(hid, weight, sizes):
+    sections, shards, heads = sizes
+    halves, count, depth = hid.shape
+    width = weight.shape[1]
+    rows = count // heads
+    bf16 = jnp.bfloat16
+    dma = pltpu.SemaphoreType.DMA
+    flops = 2 * halves * count * shards * depth * width
+    return pl.pallas_call(
+        functools.partial(project_kernel, sizes),
+        out_shape=jax.ShapeDtypeStruct((halves, shards, rows, width), bf16),
+        in_specs=[pl.BlockSpec(memory_space=pltpu.VMEM), pl.BlockSpec(memory_space=pl.ANY)],
+        out_specs=pl.BlockSpec(memory_space=pl.ANY),
+        scratch_shapes=[
+            pltpu.VMEM(weight.shape, bf16),
+            pltpu.VMEM((halves, shards - 1, count, depth), bf16),
+            pltpu.VMEM((halves, shards, heads, rows, width), bf16),
+            pltpu.VMEM((halves, shards, heads - 1, rows, width), bf16),
+            pltpu.VMEM((halves, shards, rows, width), bf16),
+            dma,
+            dma((halves, shards)),
+            dma((halves, shards)),
+            dma((halves, shards, heads)),
+            dma((halves, shards, heads)),
+            dma((halves, shards)),
+            dma((halves, shards)),
+        ],
+        compiler_params=pltpu.CompilerParams(
+            collective_id=0, has_side_effects=True, vmem_limit_bytes=48 * 2**20
+        ),
+        cost_estimate=pl.CostEstimate(
+            flops=flops, bytes_accessed=2 * weight.size, transcendentals=0
+        ),
+        name="project",
+    )(hid, weight)
 
 
 def conv_silu(padded, kernel, length):
@@ -115,19 +250,12 @@
     gated = out_ssm.reshape(length, group_count, per_group * head_dim) * gate_act
     inverse_rms = lax.rsqrt(jnp.mean(gated * gated, axis=2, keepdims=True) + epsilon)
     hidden = ((gated * inverse_rms).reshape(length, x_cols) * norm_gain[0]).astype(jnp.bfloat16)
-    local_weight = out_weight[0]
-    terms = jnp.dot(
-        lax.all_gather(hidden, "seq", axis=0, tiled=True),
-        local_weight,
-        preferred_element_type=jnp.float32,
-    )
-    shards = lax.axis_size("seq")
-    terms = terms.astype(jnp.bfloat16).reshape(shards, length, local_weight.shape[1])
-    summed = lax.psum_scatter(terms, "head", scatter_dimension=1, tiled=True)
-    spread = lax.all_to_all(summed, "seq", split_axis=0, concat_axis=2, tiled=True)
-    mixed = spread.reshape(spread.shape[1], spread.shape[2])
-    passed = passed_along_2(mixed, "section", 1)
-    return passed[None]
+    sizes = tuple(lax.axis_size(name) for name in ("section", "seq", "head"))
+    halves, heads = 2, sizes[2]
+    rows = length // (heads * halves)
+    hid = jnp.transpose(hidden.reshape(heads, halves, rows, x_cols), (1, 0, 2, 3))
+    mixed = project(hid.reshape(halves, heads * rows, x_cols), out_weight[0], sizes)
+    return jnp.transpose(mixed, (0, 2, 1, 3)).reshape(1, halves * rows, -1)
 
 
 def solution(mesh):

time: 266 us -> 214 us (0.80)
  waiting for transfers between devices: 174 us -> 39.4 us
  Pallas kernels: 0 us -> 99.7 us
  blocking collectives: 25.7 us -> 8.09 us
  matrix products: 22.9 us -> 8.66 us
  local copies, waits for them, and re-layouts: 13.5 us -> 24.5 us
    pallas_call x0 -> x1, Pallas kernels: none -> 99.7 us  [project(): pl.pallas_call(functools.partial(project_kernel, sizes), out_shape=jax.Sh...]
    reduce_scatter x1 -> x0, waiting for transfers between devices: 77 us -> none  [per_device(): summed = lax.psum_scatter(terms, 'head', scatter_dimension=1, tiled=True)]
    all_gather x1 -> x0, waiting for transfers between devices: 52.7 us -> none  [per_device(): lax.all_gather(hidden, 'seq', axis=0, tiled=True)]
    all_to_all x1 -> x0, blocking collectives: 17.6 us -> none  [per_device(): lax.all_to_all(summed, 'seq', split_axis=0, concat_axis=2, tiled=True)]
    dot_general x1 -> x0, matrix products: 13.8 us -> none  [per_device(): jnp.dot(lax.all_gather(hidden, 'seq', axis=0, tiled=True), local_weight,...]
    mul x1 -> x2, local copies, waits for them, and re-layouts: 0.61 us -> 5.99 us  [per_device(): gated * inverse_rms]
    add x0 -> x1, local copies, waits for them, and re-layouts: none -> 4.64 us  [per_device(): inside + outside]
    transpose x0 -> x1, other arithmetic: none -> 2.92 us  [per_device(): jnp.transpose(hidden.reshape(heads, halves, rows, x_cols), (1, 0, 2, 3))]
  transfers between devices with their start and end apart: 5 -> 2, of which waited for: 4 -> 1; matrix products, arithmetic and copies ran while one was open for 4% -> 6% of each run, Pallas kernels for 0% -> 0%
where the time goes in v2:
time: 214 us; the launch traced here: 212 us
  Pallas kernels  99.7 us (47%)
  waiting for transfers between devices  39.4 us (18%)
  local copies, waits for them, and re-layouts  24.5 us (11%)
  between operations  13.6 us (6%)
  other arithmetic  13.2 us (6%)
  matrix products  8.66 us (4%)
  blocking collectives  8.09 us (4%)
  starting transfers between devices  4.87 us (2%)
    pallas_call x1, Pallas kernels, project(): pl.pallas_call(functools.partial(project_kernel, sizes), out_shape=jax.Sh...  99.7 us
    all_gather x1, waiting for transfers between devices, entering(): blocks = lax.all_gather(block.astype(jnp.bfloat16), axis)  39.4 us
    all_gather x1, blocking collectives, entering(): decays = lax.all_gather(decay, axis)  8.09 us
    mul x2, local copies, waits for them, and re-layouts, per_device(): gated * inverse_rms  5.99 us
    ppermute x1, starting transfers between devices, passed_along(): return lax.ppermute(block, axis, route)  4.87 us
    add x1, local copies, waits for them, and re-layouts, per_device(): inside + outside  4.64 us
  transfers between devices with their start and end apart: 2, of which 1 were waited for; matrix products, arithmetic and copies ran while one was open for 6% of the time, Pallas kernels for 0%

profile of v2, /device:TPU:0, one launch (start us, length us, event | category | flops | bytes accessed | tf_op | source)
XLA Modules:
  0.0 212.1 jit_solution(5497385515214858057)
XLA Ops:
  6.5 0.9 slice_bitcast_fusion
  8.1 4.9 %collective-permute-start = (bf16[3,3072]{1,0:T(4,128)(2,1)S(1)}, bf16[3,3072]{1,0:T(4,128)(2,1)S(1)}, u32[]{:S(2)}, u32[]{:S(2)}) collective-permute-start(bf16[3,3072]{1,0:T(4,128)(2,1)S(1)} %pad_maximum_fusion.3), channel_id=1, source_target_pairs={{0,4},{4,8},{8,12},{1,5},{5,9},{9,13},{2,6},{6,10},{10,14},{3,7},{... | collective-permute-start | bytes 55304 | tf_op jit(solution)/shard_map/ppermute | solution.py:19
  13.0 0.9 fusion.39
  17.8 1.3 reduce.9
  19.2 0.9 multiply_bitcast_fusion
  20.0 0.9 fusion.42
  20.9 1.9 multiply_convert_fusion.6
  22.9 1.5 multiply_convert_fusion.3
  25.0 1.4 convolution_convert_fusion
  26.4 1.6 copy.71
  28.1 1.6 convert_element_type.132
  30.4 8.1 %all-gather = f32[8,16,1]{1,2,0:T(1,128)S(1)} all-gather(f32[2,16,1]{1,2,0:T(1,128)S(1)} %bitcast.92), channel_id=2, replica_groups=mesh['section'=2,'seq'=4,'head'=4] {'seq'}, dimensions={0}, use_global_device_ids=true | all-gather | bytes 640 | tf_op jit(solution)/shard_map/all_gather | solution.py:24
  39.0 1.1 fusion.29
  40.1 39.4 %all-gather.4.cloned.1.call-done = bf16[8,16,64,256]{3,2,1,0:T(8,128)(2,1)} async-done(((bf16[2,16,64,256]{3,2,1,0:T(8,128)(2,1)}), bf16[8,16,64,256]{3,2,1,0:T(8,128)(2,1)}) %all-gather.4.cloned.1.call-update) | async-done | bytes 4194320 | tf_op jit(solution)/shard_map/all_gather | solution.py:25
  79.5 3.0 %fusion.19 = f32[2,16,64,256]{3,2,1,0:T(8,128)S(1)} fusion(bf16[8,16,64,256]{3,2,1,0:T(8,128)(2,1)} %all-gather.4.cloned.1.call-done, f32[2,16]{1,0:T(2,128)S(1)} %bitcast.95, f32[2,16]{1,0:T(2,128)S(1)} %bitcast.94, f32[2,16]{1,0:T(2,128)S(1)} %bitcast.93, pred[]{:T(512)S(6)} %gt.11, pred[]{:T(512)S(6)} %gt.10, pred[]{:T(512)S(6)} %gt.9, ...), kind=kOutput, calls=%fused_computation.32 | convolution fusion | flops 274726912 | bytes 5505411 | tf_op jit(solution)/shard_map/tgn,gjpn->tgjp/dot_general | solution.py:243
  82.5 3.2 %multiply_reduce_fusion = (f32[256,2]{0,1:T(2,128)S(1)}, f32[256,2,16,64]{0,3,2,1:T(8,128)S(1)}) fusion(f32[256,2,16,64]{0,3,2,1:T(8,128)S(1)} %bitcast.69, bf16[256,2,16,64]{0,3,2,1:T(8,128)(2,1)S(1)} %bitcast.72, f32[2,16]{1,0:T(2,128)S(1)} %mul.320, f32[256,2,16]{0,2,1:T(8,128)S(1)} %get-tuple-element.7, f32[2,16,64,256]{3,2,1,0:T(8,128)S(1)} %fusion.19, ...), kind=kOutput, calls=%fused_computation.23 | convolution fusion | flops 287309312 | bytes 8030336 | tf_op jit(solution)/shard_map/gjtu,ugjp->tgjp/dot_general | solution.py:232
  85.6 4.6 %copy.70 = f32[256,2,16,64]{3,2,1,0:T(8,128)} copy(f32[256,2,16,64]{0,3,2,1:T(8,128)S(1)} %get-tuple-element.26) | data formatting | bytes 4194304 | tf_op jit(solution)/shard_map/add | solution.py:246
  90.3 3.6 %reshape.185 = f32[4,2,32,2048]{3,2,1,0:T(8,128)S(1)} reshape(f32[256,2,16,64]{3,2,1,0:T(8,128)} %copy.70) | data formatting | bytes 4194304 | tf_op jit(solution)/shard_map/reshape | solution.py:250
  94.0 1.9 mul.328
  95.9 4.1 %mul.329 = f32[4,2,32,2048]{3,2,1,0:T(8,128)} reshape(f32[256,2,1024]{2,1,0:T(2,128)} %mul.328) | data formatting | bytes 4194304 | tf_op jit(solution)/shard_map/mul | solution.py:252
  100.0 2.9 %fusion.24 = bf16[2,4,32,2048]{3,2,0,1:T(8,128)(2,1)S(1)} fusion(f32[2048]{0:T(1024)S(1)} %bitcast.91, f32[4,2,32,2048]{3,2,1,0:T(8,128)} %mul.329, f32[4,2,32,2048]{3,2,1,0:T(8,128)S(1)} %reshape.185, f32[4,2,32,2048]{3,2,1,0:T(8,128)} %bitcast.66), kind=kLoop, calls=%fused_computation.36 | loop fusion | flops 4194304 | bytes 7348224 | tf_op jit(solution)/shard_map/transpose | solution.py:256
  103.1 99.7 %project.1 = bf16[2,4,32,2048]{3,2,1,0:T(8,128)(2,1)S(1)} custom-call(bf16[2,128,2048]{2,1,0:T(8,128)(2,1)S(1)} %bitcast.64, bf16[2048,2048]{1,0:T(8,128)(2,1)} %bitcast.97), custom_call_target="tpu_custom_call" | custom-call | flops 8589934592 | bytes 8388608 | tf_op jit(solution)/shard_map/project/pallas_call | solution.py:141
  202.8 0.8 copy.74
  203.6 1.6 reshape.187
  (50 shorter events, 6.7 us)
Async XLA Ops:
  6.5 16.4 %copy-start.2 = (bf16[1,256,2048]{2,1,0:T(8,128)(2,1)S(1)}, bf16[1,256,2048]{2,1,0:T(8,128)(2,1)}, u32[]{:S(2)}) copy-start(bf16[1,256,2048]{2,1,0:T(8,128)(2,1)} %param.13) | copy-start | bytes 3145732
  6.5 72.9 %all-gather.4.cloned.1.call-start = ((), (), s32[]{:S(2)}) async-start(), calls=%async_computation | async-start | bytes 5242880 | tf_op jit(solution)/shard_map/all_gather | solution.py:25
  8.1 12.8 %collective-permute-start = (bf16[3,3072]{1,0:T(4,128)(2,1)S(1)}, bf16[3,3072]{1,0:T(4,128)(2,1)S(1)}, u32[]{:S(2)}, u32[]{:S(2)}) collective-permute-start(bf16[3,3072]{1,0:T(4,128)(2,1)S(1)} %pad_maximum_fusion.3), channel_id=1, source_target_pairs={{0,4},{4,8},{8,12},{1,5},{5,9},{9,13},{2,6},{6,10},{10,14},{3,7},{... | collective-permute-start | bytes 55304 | tf_op jit(solution)/shard_map/ppermute | solution.py:19
  25.0 1.5 copy-start
  28.1 1.6 copy-start.7
  28.1 10.4 %copy-start.5 = (f32[1,4,512]{2,1,0:T(4,128)S(1)}, f32[1,4,512]{2,1,0:T(4,128)}, u32[]{:S(2)}) copy-start(f32[1,4,512]{2,1,0:T(4,128)} %param.20) | copy-start | bytes 24580
  28.1 10.4 %copy-start.4 = (bf16[1,256,512]{2,1,0:T(8,128)(2,1)S(1)}, bf16[1,256,512]{2,1,0:T(8,128)(2,1)}, u32[]{:S(2)}) copy-start(bf16[1,256,512]{2,1,0:T(8,128)(2,1)} %param.15) | copy-start | bytes 786436
  79.5 3.0 %copy-start.1 = (f32[1,256,2048]{1,2,0:T(8,128)S(1)}, f32[1,256,2048]{1,2,0:T(8,128)}, u32[]{:S(2)}) copy-start(f32[1,256,2048]{1,2,0:T(8,128)} %copy.71) | copy-start | bytes 6291460
  79.5 3.0 %copy-start.3 = (f32[2,256,256]{2,1,0:T(8,128)S(1)}, f32[2,256,256]{2,1,0:T(8,128)}, u32[]{:S(2)}) copy-start(f32[2,256,256]{2,1,0:T(8,128)} %fusion.29) | copy-start | bytes 1572868
  95.9 4.1 %copy-start.6 = (f32[1,2048]{1,0:T(1,128)S(1)}, f32[1,2048]{1,0:T(1,128)}, u32[]{:S(2)}) copy-start(f32[1,2048]{1,0:T(1,128)} %param.24) | copy-start | bytes 24580
Sparse Core Ops, SparseCore 0:
  26.5 52.8 all-gather.3
